TPU v7x, 128 devices: a whole 4x4x4 slice. The times are simulated.
128 devices in a mesh: rep: 1, dp: 128 (over x, y, z, core).
Axes of the slice: x: 4, y: 4, z: 4, core: 2. Of those that a mesh axis runs over, the one named last changes fastest.
Arguments:
- a: bfloat16 [128, 2, 4096, 1024], P(('rep', 'dp'))
- g: bfloat16 [128, 2, 4096, 3328], P(('rep', 'dp'))
Outputs:
- output: bfloat16 [2, 1024, 3328], P('rep')
All inputs are finite; a program needn't handle non-finite values.
Results may differ from a plain program's by a relative error of at most 0.012.
Values are sent between devices in bfloat16 or wider.
A program may use at most 1.5 GiB of HBM per device.

v0:
```python
import jax
import jax.numpy as jnp


def solution(mesh):
    groups = mesh.shape["rep"]

    def step(a, g):
        a, g = (t.reshape(groups, -1, *t.shape[1:]) for t in (a, g))
        sums = jnp.einsum("rsntd,rsntf->rndf", a, g, preferred_element_type=jnp.float32)
        return sums.astype(jnp.bfloat16).reshape(-1, *sums.shape[2:])

    return step
```

profile of v0, /device:TPU:1, one launch (start us, length us, event | category | flops | bytes accessed | tf_op | source)
XLA Modules:
  0.0 240.2 jit_solution(5768762122736656967)
XLA Ops:
  0.0 68.6 %fusion = f32[2,1024,3328]{2,1,0:T(8,128)} fusion(bf16[1,2,4096,3328]{3,2,1,0:T(8,128)(2,1)} %param.1, bf16[1,2,4096,1024]{3,2,1,0:T(8,128)(2,1)} %param), kind=kOutput, calls=%fused_computation | convolution fusion | flops 55834574848 | bytes 98566144 | tf_op jit(solution)/rsntd,rsntf->rndf/dot_general | solution.py:10
  68.6 171.6 %all-reduce.2 = bf16[2,1024,3328]{2,1,0:T(8,128)(2,1)} all-reduce(f32[2,1024,3328]{2,1,0:T(8,128)} %fusion), channel_id=1, replica_groups=mesh['axis_0'=128] {'axis_0'}, use_global_device_ids=true, to_apply=%add.clone | all-reduce | flops 6815744 | bytes 40894464 | tf_op jit(solution)/rsntd,rsntf->rndf/dot_general | solution.py:10
where the time goes:
time: 242 us; the launch traced here: 240 us
  blocking collectives  172 us (71%)
  matrix products  68.6 us (28%)
    dot_general x1, blocking collectives, step(): jnp.einsum('rsntd,rsntf->rndf', a, g, preferred_element_type=jnp.float32)  172 us
    dot_general x1, matrix products, step(): jnp.einsum('rsntd,rsntf->rndf', a, g, preferred_element_type=jnp.float32)  68.6 us

commit v1 on v0

v1 whole, which is shorter than its diff:
```python
import jax
import jax.numpy as jnp
from jax import lax
from jax.experimental import pallas as pl
from jax.experimental.pallas import tpu as pltpu
from jax.sharding import PartitionSpec as P

MATRICES, TOKENS, D, FF = 2, 4096, 1024, 3328
WIDTH = 256
PER = FF // WIDTH
UNITS = MATRICES * PER
CHUNK = 512
CHUNKS = TOKENS // CHUNK
BF, F32 = jnp.bfloat16, jnp.float32
AT = (1, 3, 5, 7, 9, 10, 11, 12, 14, 16, 18)
DEPTH = AT[-1]


def kernel(
    a_ref, g_ref, out_ref,
    at_ref, araw, gbuf, tb, rp, r1, x1, s2, r2, x2, s3, r3,
    a_sem, g_sem, o_sem, pair_send, pair_recv, back_recv, send_sem, recv1, recv2, recv3, back1, back2, back3,
):
    me = lax.axis_index("dp")
    core = lax.rem(me, 2)
    partner = me + 1 - 2 * core
    cx, cy, cz = lax.div(me, 32), lax.rem(lax.div(me, 8), 4), lax.rem(lax.div(me, 2), 4)

    def to(device):
        return {"device_id": {"dp": device}, "device_id_type": pl.DeviceIdType.MESH}

    def remote(src, dst, ssem, rsem, device):
        return pltpu.make_async_remote_copy(src_ref=src, dst_ref=dst, send_sem=ssem, recv_sem=rsem, **to(device))

    def wait_for(ref, sem):
        pltpu.make_async_copy(ref, ref, sem).wait()

    def along(m, stride, off):
        return me + (lax.rem(m + off + 4, 4) - m) * stride

    barrier = pltpu.get_barrier_semaphore()
    pl.semaphore_signal(barrier, inc=1, **to(partner))
    for m, stride in ((cx, 32), (cy, 8), (cz, 2)):
        for off in (1, 2, 3):
            pl.semaphore_signal(barrier, inc=1, **to(along(m, stride, off)))

    def a_copy(n, k, slot):
        return pltpu.make_async_copy(a_ref.at[0, n, pl.ds(k * CHUNK, CHUNK)], araw.at[slot], a_sem.at[slot])

    def g_copy(u, slot):
        n = lax.div(u, PER)
        col = pl.multiple_of((u - n * PER) * WIDTH, WIDTH)
        return pltpu.make_async_copy(g_ref.at[0, n, :, pl.ds(col, WIDTH)], gbuf.at[slot], g_sem.at[slot])

    a_copy(0, 0, 0).start()
    a_copy(0, 1, 1).start()
    g_copy(0, 0).start()

    def turn(n, k, slot):
        at_ref[n, :, pl.ds(pl.multiple_of(k * CHUNK, CHUNK), CHUNK)] = araw[slot].T

    def first(k, _):
        slot = lax.rem(k, 2)
        a_copy(0, k, slot).wait()
        turn(0, k, slot)

        @pl.when(k < CHUNKS - 2)
        def _():
            a_copy(0, k + 2, slot).start()

        return 0

    lax.fori_loop(0, CHUNKS, first, 0)
    a_copy(1, 0, 0).start()
    a_copy(1, 1, 1).start()
    pl.semaphore_wait(barrier, 10)

    def place(u):
        k = lax.rem(u, 3)
        e0, e1, e2 = lax.div((1 - k) * (2 - k), 2), k * (2 - k), lax.div(k * (k - 1), 2)
        dims = ((cx, 32), (cy, 8), (cz, 2))
        res = []
        for p in range(3):
            (ma, sa), (mb, sb), (mc, sc) = dims[p], dims[(p + 1) % 3], dims[(p + 2) % 3]
            res.append((e0 * ma + e1 * mb + e2 * mc, e0 * sa + e1 * sb + e2 * sc))
        return res

    def way(u):
        return 1 - 2 * lax.rem(lax.div(u, 3), 2)

    def term(u, rows):
        return tb[u, core, rows].astype(F32)

    def events(t):
        def at(stage):
            return t - AT[stage]

        def on(stage):
            def wrap(f):
                u = at(stage)
                pl.when((u >= 0) & (u < UNITS))(lambda: f(u))

            return wrap

        @on(0)
        def _(u):
            (m, stride), _, _ = place(u)
            s = way(u)
            wait_for(rp.at[u], pair_recv.at[u])
            wait_for(rp.at[u], pair_send.at[u])
            for i, (q, off) in enumerate(((m + 2, s), (m - s, -s))):
                rows = pl.ds(lax.rem(q + 4, 4) * 16, 16)
                rp[u, rows] = (term(u, rows) + rp[u, rows].astype(F32)).astype(BF)
                remote(rp.at[u, rows], r1.at[u, i], send_sem.at[u], recv1.at[u, i], along(m, stride, off)).start()

        @on(1)
        def _(u):
            (m, stride), _, _ = place(u)
            s = way(u)
            wait_for(r1.at[u, 0], recv1.at[u, 0])
            rows = pl.ds(lax.rem(m + s + 4, 4) * 16, 16)
            rp[u, rows] = (term(u, rows) + rp[u, rows].astype(F32) + r1[u, 0].astype(F32)).astype(BF)
            remote(rp.at[u, rows], r1.at[u, 2], send_sem.at[u], recv1.at[u, 2], along(m, stride, s)).start()

        @on(2)
        def _(u):
            (m1, _), (m, stride), _ = place(u)
            wait_for(r1.at[u, 1], recv1.at[u, 1])
            wait_for(r1.at[u, 2], recv1.at[u, 2])
            rows = pl.ds(m1 * 16, 16)
            x1[u] = (term(u, rows) + rp[u, rows].astype(F32)) + (r1[u, 1].astype(F32) + r1[u, 2].astype(F32))
            for i in range(3):
                off = i + 1
                s2[u, i] = x1[u, pl.ds(lax.rem(m + off, 4) * 4, 4)].astype(BF)
                remote(s2.at[u, i], r2.at[u, i], send_sem.at[u], recv2.at[u, i], along(m, stride, off)).start()

        @on(3)
        def _(u):
            _, (m2, _), (m, stride) = place(u)
            for i in range(3):
                wait_for(r2.at[u, i], recv2.at[u, i])
            x2[u] = (x1[u, pl.ds(m2 * 4, 4)] + r2[u, 0].astype(F32)) + (r2[u, 1].astype(F32) + r2[u, 2].astype(F32))
            for i in range(3):
                off = i + 1
                s3[u, i] = x2[u, pl.ds(lax.rem(m + off, 4), 1)].astype(BF)
                remote(s3.at[u, i], r3.at[u, i], send_sem.at[u], recv3.at[u, i], along(m, stride, off)).start()

        @on(4)
        def _(u):
            (m1, _), (m2, _), (m, stride) = place(u)
            for i in range(3):
                wait_for(r3.at[u, i], recv3.at[u, i])
            rows = pl.ds(m1 * 16 + m2 * 4 + m, 1)
            tb[u, core, rows] = (
                (x2[u, pl.ds(m, 1)] + r3[u, 0].astype(F32)) + (r3[u, 1].astype(F32) + r3[u, 2].astype(F32))
            ).astype(BF)
            for i in range(3):
                block = tb.at[u, core, rows]
                remote(block, block, send_sem.at[u], back3.at[u, i], along(m, stride, i + 1)).start()

        @on(5)
        def _(u):
            (m1, _), (m, stride), _ = place(u)
            for i in range(3):
                wait_for(tb.at[u, 0, pl.ds(0, 1)], back3.at[u, i])
            block = tb.at[u, core, pl.ds(m1 * 16 + m * 4, 4)]
            for i in range(3):
                remote(block, block, send_sem.at[u], back2.at[u, i], along(m, stride, i + 1)).start()

        @on(6)
        def _(u):
            (m, stride), _, _ = place(u)
            s = way(u)
            for i in range(3):
                wait_for(tb.at[u, 0, pl.ds(0, 4)], back2.at[u, i])
            block = tb.at[u, core, pl.ds(m * 16, 16)]
            for i, off in enumerate((s, -s)):
                remote(block, block, send_sem.at[u], back1.at[u, i], along(m, stride, off)).start()

        @on(7)
        def _(u):
            (m, stride), _, _ = place(u)
            s = way(u)
            wait_for(tb.at[u, 0, pl.ds(0, 16)], back1.at[u, 0])
            block = tb.at[u, core, pl.ds(lax.rem(m - s + 4, 4) * 16, 16)]
            remote(block, block, send_sem.at[u], back1.at[u, 2], along(m, stride, s)).start()

        @on(8)
        def _(u):
            wait_for(tb.at[u, 0, pl.ds(0, 16)], back1.at[u, 1])
            wait_for(tb.at[u, 0, pl.ds(0, 16)], back1.at[u, 2])
            block = tb.at[u, core]
            remote(block, block, send_sem.at[u], back_recv.at[u], partner).start()

        @on(9)
        def _(u):
            wait_for(tb.at[u, 0], back_recv.at[u])
            n = lax.div(u, PER)
            for h in range(2):
                col = pl.multiple_of((u - n * PER) * WIDTH + h * 128, 128)
                pltpu.make_async_copy(tb.at[u, h], out_ref.at[n, :, :, pl.ds(col, 128)], o_sem.at[u]).start()

        @on(10)
        def _(u):
            wait_for(tb.at[u], o_sem.at[u])
            wait_for(gbuf.at[0, pl.ds(0, 190 * 8)], send_sem.at[u])

    def loop(t, _):
        n = lax.div(t, PER)
        slot = lax.rem(t, 2)
        g_copy(t, slot).wait()

        @pl.when(t < UNITS - 1)
        def _():
            g_copy(t + 1, 1 - slot).start()

        acc = lax.dot_general(
            at_ref[n], gbuf[slot], (((1,), (0,)), ((), ())), preferred_element_type=F32
        ).astype(BF)
        for h in range(2):
            tb[t, h] = acc[:, h * 128 : (h + 1) * 128].reshape(64, 16, 128)
        remote(tb.at[t, 1 - core], rp.at[t], pair_send.at[t], pair_recv.at[t], partner).start()

        @pl.when(t < CHUNKS)
        def _():
            a_copy(1, t, slot).wait()
            turn(1, t, slot)

            @pl.when(t < CHUNKS - 2)
            def _():
                a_copy(1, t + 2, slot).start()

        events(t)
        return 0

    lax.fori_loop(0, UNITS, loop, 0)
    lax.fori_loop(UNITS, UNITS + DEPTH, lambda t, _: (events(t), 0)[1], 0)


def solution(mesh):
    dma, tile = pltpu.SemaphoreType.DMA, (16, 128)

    def body(a, g):
        out = pl.pallas_call(
            kernel,
            out_shape=jax.ShapeDtypeStruct((MATRICES, D // 16, 16, FF), BF),
            in_specs=[pl.BlockSpec(memory_space=pl.ANY)] * 2,
            out_specs=pl.BlockSpec(memory_space=pl.ANY),
            scratch_shapes=[
                pltpu.VMEM((MATRICES, D, TOKENS), BF),
                pltpu.VMEM((2, CHUNK, D), BF),
                pltpu.VMEM((2, TOKENS, WIDTH), BF),
                pltpu.VMEM((UNITS, 2, 64, *tile), BF),
                pltpu.VMEM((UNITS, 64, *tile), BF),
                pltpu.VMEM((UNITS, 3, 16, *tile), BF),
                pltpu.VMEM((UNITS, 16, *tile), F32),
                pltpu.VMEM((UNITS, 3, 4, *tile), BF),
                pltpu.VMEM((UNITS, 3, 4, *tile), BF),
                pltpu.VMEM((UNITS, 4, *tile), F32),
                pltpu.VMEM((UNITS, 3, 1, *tile), BF),
                pltpu.VMEM((UNITS, 3, 1, *tile), BF),
                dma((2,)),
                dma((2,)),
                dma((UNITS,)),
                dma((UNITS,)),
                dma((UNITS,)),
                dma((UNITS,)),
                dma((UNITS,)),
                *[dma((UNITS, 3))] * 6,
            ],
            compiler_params=pltpu.CompilerParams(
                collective_id=0, has_side_effects=True, vmem_limit_bytes=67043328
            ),
            cost_estimate=pl.CostEstimate(
                flops=2 * MATRICES * TOKENS * D * FF, bytes_accessed=100_000_000, transcendentals=0
            ),
        )(a, g)
        return out.reshape(MATRICES, D, FF)

    return jax.shard_map(
        body,
        mesh=mesh,
        in_specs=(P(("rep", "dp")), P(("rep", "dp"))),
        out_specs=P("rep"),
        check_vma=False,
    )
```

time: 242 us -> 163 us (0.67)
  blocking collectives: 172 us -> 0 us
  Pallas kernels: 0 us -> 151 us
  matrix products: 68.6 us -> 0 us
  local copies, waits for them, and re-layouts: 0 us -> 12.1 us
    dot_general x1 -> x0, blocking collectives: 172 us -> none  [step(): jnp.einsum('rsntd,rsntf->rndf', a, g, preferred_element_type=jnp.float32)]
    pallas_call x0 -> x1, Pallas kernels: none -> 151 us  [body(): pl.pallas_call(kernel, out_shape=jax.ShapeDtypeStruct((MATRICES, D // 16,...]
    dot_general x1 -> x0, matrix products: 68.6 us -> none  [step(): jnp.einsum('rsntd,rsntf->rndf', a, g, preferred_element_type=jnp.float32)]
    unnamed x0 -> x1, local copies, waits for them, and re-layouts: none -> 12.1 us
where the time goes in v1:
time: 163 us
  Pallas kernels  151 us (93%)
  local copies, waits for them, and re-layouts  12.1 us (7%)
    pallas_call x1, Pallas kernels, body(): pl.pallas_call(kernel, out_shape=jax.ShapeDtypeStruct((MATRICES, D // 16,...  151 us
    unnamed x1, local copies, waits for them, and re-layouts  12.1 us

profile of v1, /device:TPU:1, one launch (start us, length us, event | category | flops | bytes accessed | tf_op | source)
XLA Modules:
  0.0 163.0 jit_solution(11729692050245937421)
XLA Ops:
  0.0 150.8 %shard_map.28 = bf16[2,64,16,3328]{3,2,1,0:T(8,128)(2,1)} custom-call(bf16[1,2,4096,1024]{3,2,1,0:T(8,128)(2,1)} %a_ref.1, bf16[1,2,4096,3328]{3,2,1,0:T(8,128)(2,1)} %g_ref.1), custom_call_target="tpu_custom_call" | custom-call | flops 55834574848 | bytes 100000000 | tf_op jit(solution)/shard_map/pallas_call | solution.py:244
  150.9 12.1 %copy.4 = bf16[2,1024,3328]{2,1,0:T(8,128)(2,1)} copy(bf16[2,1024,3328]{2,1,0:T(8,128)(2,1)} %bitcast.1) | data formatting | bytes 27262976

commit v2 on v1

v2 whole, which is shorter than its diff:
```python
import jax
import jax.numpy as jnp
from jax import lax
from jax.experimental import pallas as pl
from jax.experimental.pallas import tpu as pltpu
from jax.sharding import PartitionSpec as P

MATRICES, TOKENS, D, FF = 2, 4096, 1024, 3328
WIDTH = 256
PER = FF // WIDTH
UNITS = MATRICES * PER
CHUNK = 512
CHUNKS = TOKENS // CHUNK
BF, F32 = jnp.bfloat16, jnp.float32
DIRECT = 20
RELAYED = (1, 3, 5, 7, 9, 11, 13, 15, 17, 18)
STRAIGHT = (1, None, 3, 5, 7, 9, 11, None, 13, 14)
LAST = UNITS - 1 + STRAIGHT[-1]


def kernel(
    a_ref, g_ref, tb,
    at_ref, araw, gbuf, total, rp, r1, x1, s2, r2, x2, s3, r3,
    a_sem, g_sem, pair_send, pair_recv, back_recv, send_sem, far1, recv1, recv2, recv3, over1, back1, back2, back3,
):
    me = lax.axis_index("dp")
    core = lax.rem(me, 2)
    partner = me + 1 - 2 * core
    cx, cy, cz = lax.div(me, 32), lax.rem(lax.div(me, 8), 4), lax.rem(lax.div(me, 2), 4)

    def to(device):
        return {"device_id": {"dp": device}, "device_id_type": pl.DeviceIdType.MESH}

    def remote(src, dst, ssem, rsem, device):
        return pltpu.make_async_remote_copy(src_ref=src, dst_ref=dst, send_sem=ssem, recv_sem=rsem, **to(device))

    def wait_for(ref, sem):
        pltpu.make_async_copy(ref, ref, sem).wait()

    def along(m, stride, off):
        return me + (lax.rem(m + off + 4, 4) - m) * stride

    barrier = pltpu.get_barrier_semaphore()
    pl.semaphore_signal(barrier, inc=1, **to(partner))
    for m, stride in ((cx, 32), (cy, 8), (cz, 2)):
        for off in (1, 2, 3):
            pl.semaphore_signal(barrier, inc=1, **to(along(m, stride, off)))

    def a_copy(n, k, slot):
        return pltpu.make_async_copy(a_ref.at[0, n, pl.ds(k * CHUNK, CHUNK)], araw.at[slot], a_sem.at[slot])

    def g_copy(u, slot):
        n = lax.div(u, PER)
        col = pl.multiple_of((u - n * PER) * WIDTH, WIDTH)
        return pltpu.make_async_copy(g_ref.at[0, n, :, pl.ds(col, WIDTH)], gbuf.at[slot], g_sem.at[slot])

    a_copy(0, 0, 0).start()
    a_copy(0, 1, 1).start()
    g_copy(0, 0).start()

    def turned(slot):
        return araw[slot].T

    def piece(k):
        return pl.ds(pl.multiple_of(k * CHUNK, CHUNK), CHUNK)

    def product(left, right):
        return lax.dot_general(left, right, (((1,), (0,)), ((), ())), preferred_element_type=F32)

    g_copy(0, 0).wait()
    g_copy(1, 1).start()
    total[...] = jnp.zeros_like(total)

    def first(k, _):
        slot = lax.rem(k, 2)
        a_copy(0, k, slot).wait()
        block = turned(slot)
        at_ref[0, :, piece(k)] = block
        total[...] += product(block, gbuf[0, piece(k)])
        a_copy(lax.div(k, CHUNKS - 2), lax.rem(k + 2, CHUNKS), slot).start()
        return 0

    lax.fori_loop(0, CHUNKS, first, 0)
    pl.semaphore_wait(barrier, 10)

    def keep(t, acc):
        acc = acc.astype(BF)
        for h in range(2):
            tb[t, h] = acc[:, h * 128 : (h + 1) * 128].reshape(64, 16, 128)
        remote(tb.at[t, 1 - core], rp.at[t], pair_send.at[t], pair_recv.at[t], partner).start()

    keep(0, total[...])

    def place(u):
        k = lax.rem(u, 3)
        e0, e1, e2 = lax.div((1 - k) * (2 - k), 2), k * (2 - k), lax.div(k * (k - 1), 2)
        dims = ((cx, 32), (cy, 8), (cz, 2))
        res = []
        for p in range(3):
            (ma, sa), (mb, sb), (mc, sc) = dims[p], dims[(p + 1) % 3], dims[(p + 2) % 3]
            res.append((e0 * ma + e1 * mb + e2 * mc, e0 * sa + e1 * sb + e2 * sc))
        return res

    def way(u):
        return 1 - 2 * lax.rem(lax.div(u, 3), 2)

    def term(u, rows):
        return tb[u, core, rows].astype(F32)

    def events(t, straight, lo=0, hi=99):
        stages = STRAIGHT if straight else RELAYED
        begin, end = (DIRECT, UNITS) if straight else (0, DIRECT)

        def on(stage):
            def wrap(f):
                if stages[stage] is None or not lo <= stages[stage] <= hi:
                    return
                u = t - stages[stage]
                pl.when((u >= begin) & (u < end))(lambda: f(u))

            return wrap

        @on(0)
        def _(u):
            (m, stride), _, _ = place(u)
            s = way(u)
            wait_for(rp.at[u], pair_recv.at[u])
            wait_for(rp.at[u], pair_send.at[u])

            def send(i, q, off, sem):
                rows = pl.ds(lax.rem(q + 4, 4) * 16, 16)
                rp[u, rows] = (term(u, rows) + rp[u, rows].astype(F32)).astype(BF)
                remote(rp.at[u, rows], r1.at[u, i], send_sem.at[u], sem.at[u], along(m, stride, off)).start()

            if straight:
                send(0, m + 2, 2, recv1)
                send(1, m - s, -s, recv1)
                send(2, m + s, s, recv1)
            else:
                send(0, m + 2, s, far1)
                send(1, m - s, -s, recv1)

        @on(1)
        def _(u):
            (m, stride), _, _ = place(u)
            s = way(u)
            wait_for(r1.at[u, 0], far1.at[u])
            rows = pl.ds(lax.rem(m + s + 4, 4) * 16, 16)
            rp[u, rows] = (term(u, rows) + rp[u, rows].astype(F32) + r1[u, 0].astype(F32)).astype(BF)
            remote(rp.at[u, rows], r1.at[u, 2], send_sem.at[u], recv1.at[u], along(m, stride, s)).start()

        @on(2)
        def _(u):
            (m1, _), (m, stride), _ = place(u)
            rows = pl.ds(m1 * 16, 16)
            came = r1.at[u] if straight else r1.at[u, pl.ds(1, 2)]
            wait_for(came, recv1.at[u])
            got = r1[u, 1].astype(F32) + r1[u, 2].astype(F32)
            if straight:
                got += r1[u, 0].astype(F32)
            x1[u] = (term(u, rows) + rp[u, rows].astype(F32)) + got
            for i in range(3):
                off = i + 1
                s2[u, i] = x1[u, pl.ds(lax.rem(m + off, 4) * 4, 4)].astype(BF)
                remote(s2.at[u, i], r2.at[u, i], send_sem.at[u], recv2.at[u], along(m, stride, off)).start()

        @on(3)
        def _(u):
            _, (m2, _), (m, stride) = place(u)
            wait_for(r2.at[u], recv2.at[u])
            x2[u] = (x1[u, pl.ds(m2 * 4, 4)] + r2[u, 0].astype(F32)) + (r2[u, 1].astype(F32) + r2[u, 2].astype(F32))
            for i in range(3):
                off = i + 1
                s3[u, i] = x2[u, pl.ds(lax.rem(m + off, 4), 1)].astype(BF)
                remote(s3.at[u, i], r3.at[u, i], send_sem.at[u], recv3.at[u], along(m, stride, off)).start()

        @on(4)
        def _(u):
            (m1, _), (m2, _), (m, stride) = place(u)
            wait_for(r3.at[u], recv3.at[u])
            rows = pl.ds(m1 * 16 + m2 * 4 + m, 1)
            tb[u, core, rows] = (
                (x2[u, pl.ds(m, 1)] + r3[u, 0].astype(F32)) + (r3[u, 1].astype(F32) + r3[u, 2].astype(F32))
            ).astype(BF)
            for i in range(3):
                block = tb.at[u, core, rows]
                remote(block, block, send_sem.at[u], back3.at[u], along(m, stride, i + 1)).start()

        @on(5)
        def _(u):
            (m1, _), (m, stride), _ = place(u)
            wait_for(tb.at[u, 0, pl.ds(0, 3)], back3.at[u])
            block = tb.at[u, core, pl.ds(m1 * 16 + m * 4, 4)]
            for i in range(3):
                remote(block, block, send_sem.at[u], back2.at[u], along(m, stride, i + 1)).start()

        @on(6)
        def _(u):
            (m, stride), _, _ = place(u)
            s = way(u)
            wait_for(tb.at[u, 0, pl.ds(0, 12)], back2.at[u])
            block = tb.at[u, core, pl.ds(m * 16, 16)]

            def send(off, sem):
                remote(block, block, send_sem.at[u], sem.at[u], along(m, stride, off)).start()

            if straight:
                send(2, back1)
                send(1, back1)
                send(3, back1)
            else:
                send(s, over1)
                send(-s, back1)

        @on(7)
        def _(u):
            (m, stride), _, _ = place(u)
            s = way(u)
            wait_for(tb.at[u, 0, pl.ds(0, 16)], over1.at[u])
            block = tb.at[u, core, pl.ds(lax.rem(m - s + 4, 4) * 16, 16)]
            remote(block, block, send_sem.at[u], back1.at[u], along(m, stride, s)).start()

        @on(8)
        def _(u):
            wait_for(tb.at[u, 0, pl.ds(0, 48 if straight else 32)], back1.at[u])
            block = tb.at[u, core]
            remote(block, block, send_sem.at[u], back_recv.at[u], partner).start()

        @on(9)
        def _(u):
            wait_for(tb.at[u, 0], back_recv.at[u])
            wait_for(gbuf.at[0, pl.ds(0, 190 * 8)], send_sem.at[u])

    def loop(t, turning, lo, hi):
        slot = lax.rem(t, 2)
        g_copy(t, slot).wait()

        @pl.when(t < UNITS - 1)
        def _():
            g_copy(t + 1, 1 - slot).start()

        if turning:
            k = t - 1
            half = lax.rem(k, 2)
            a_copy(1, k, half).wait()
            acc = product(at_ref[0], gbuf[slot])
            at_ref[1, :, piece(k)] = turned(half)
            keep(t, acc)

            @pl.when(k < CHUNKS - 2)
            def _():
                a_copy(1, k + 2, half).start()

        else:
            keep(t, product(at_ref[lax.div(t, PER)], gbuf[slot]))
        events(t, False, lo, hi)
        if hi > CHUNKS:
            pl.when(t > DIRECT)(lambda: events(t, True, 0, UNITS - 1 - DIRECT))
        return 0

    def tail(t, _):
        events(t, False, UNITS - DIRECT + 1, 99)
        events(t, True)
        return 0

    lax.fori_loop(1, CHUNKS + 1, lambda t, _: loop(t, True, 0, CHUNKS), 0)
    lax.fori_loop(CHUNKS + 1, UNITS, lambda t, _: loop(t, False, 0, 99), 0)
    lax.fori_loop(UNITS, LAST + 1, tail, 0)


def write(tb, out_ref, sem):
    copies = []
    for n in range(MATRICES):
        for j in range(PER):
            for h in range(2):
                block = out_ref.at[n, :, :, pl.ds(j * WIDTH + h * 128, 128)]
                copies.append(pltpu.make_async_copy(tb.at[n * PER + j, h], block, sem.at[n, j, h]))
    for copy in copies:
        copy.start()
    for copy in copies:
        copy.wait()


def solution(mesh):
    dma, tile = pltpu.SemaphoreType.DMA, (16, 128)

    def body(a, g):
        out = pl.pallas_call(
            kernel,
            out_shape=pltpu.VMEM((UNITS, 2, 64, *tile), BF),
            in_specs=[pl.BlockSpec(memory_space=pl.ANY)] * 2,
            out_specs=pl.BlockSpec(memory_space=pltpu.VMEM),
            scratch_shapes=[
                pltpu.VMEM((MATRICES, D, TOKENS), BF),
                pltpu.VMEM((2, CHUNK, D), BF),
                pltpu.VMEM((2, TOKENS, WIDTH), BF),
                pltpu.VMEM((D, WIDTH), F32),
                pltpu.VMEM((UNITS, 64, *tile), BF),
                pltpu.VMEM((UNITS, 3, 16, *tile), BF),
                pltpu.VMEM((UNITS, 16, *tile), F32),
                pltpu.VMEM((UNITS, 3, 4, *tile), BF),
                pltpu.VMEM((UNITS, 3, 4, *tile), BF),
                pltpu.VMEM((UNITS, 4, *tile), F32),
                pltpu.VMEM((UNITS, 3, 1, *tile), BF),
                pltpu.VMEM((UNITS, 3, 1, *tile), BF),
                dma((2,)),
                dma((2,)),
                *[dma((UNITS,))] * 12,
            ],
            compiler_params=pltpu.CompilerParams(
                collective_id=0, has_side_effects=True, vmem_limit_bytes=50 << 20
            ),
            cost_estimate=pl.CostEstimate(
                flops=2 * MATRICES * TOKENS * D * FF, bytes_accessed=100_000_000, transcendentals=0
            ),
        )(a, g)
        out = pl.pallas_call(
            write,
            out_shape=jax.ShapeDtypeStruct((MATRICES, D // 16, 16, FF), BF),
            in_specs=[pl.BlockSpec(memory_space=pltpu.VMEM)],
            out_specs=pl.BlockSpec(memory_space=pl.ANY),
            scratch_shapes=[dma((MATRICES, PER, 2))],
            compiler_params=pltpu.CompilerParams(vmem_limit_bytes=1 << 20),
        )(pltpu.with_memory_space_constraint(out, pltpu.VMEM))
        return out.reshape(MATRICES, D, FF)

    return jax.shard_map(
        body,
        mesh=mesh,
        in_specs=(P(("rep", "dp")), P(("rep", "dp"))),
        out_specs=P("rep"),
        check_vma=False,
    )
```

time: 163 us -> 125 us (0.77)
  Pallas kernels: 151 us -> 125 us
  local copies, waits for them, and re-layouts: 12.1 us -> 0 us
    pallas_call x1 -> x2, Pallas kernels: 151 us -> 125 us  [the longest x1 120 us: body(): pl.pallas_call(kernel, out_shape=pltpu.VMEM((UNITS, 2, 64, *tile), BF), i...]
    unnamed x1 -> x0, local copies, waits for them, and re-layouts: 12.1 us -> none
where the time goes in v2:
time: 125 us
  Pallas kernels  125 us (100%)
    pallas_call x1, Pallas kernels, body(): pl.pallas_call(kernel, out_shape=pltpu.VMEM((UNITS, 2, 64, *tile), BF), i...  120 us
    pallas_call x1, Pallas kernels, body(): pl.pallas_call(write, out_shape=jax.ShapeDtypeStruct((MATRICES, D // 16,...  5.29 us

profile of v2, /device:TPU:1, one launch (start us, length us, event | category | flops | bytes accessed | tf_op | source)
XLA Modules:
  0.0 125.2 jit_solution(15466757660167868940)
XLA Ops:
  0.0 119.9 %shard_map.28.tb = bf16[26,2,64,16,128]{4,3,2,1,0:T(8,128)(2,1)S(1)} custom-call(bf16[1,2,4096,1024]{3,2,1,0:T(8,128)(2,1)} %a_ref.1, bf16[1,2,4096,3328]{3,2,1,0:T(8,128)(2,1)} %g_ref.1), custom_call_target="tpu_custom_call" | custom-call | flops 55834574848 | bytes 100000000 | tf_op jit(solution)/shard_map/pallas_call | solution.py:288
  120.0 5.3 %shard_map.29 = bf16[2,64,16,3328]{3,2,1,0:T(8,128)(2,1)} custom-call(bf16[26,2,64,16,128]{4,3,2,1,0:T(8,128)(2,1)S(1)} %shard_map.28.tb), custom_call_target="tpu_custom_call" | custom-call | tf_op jit(solution)/shard_map/pallas_call | solution.py:317

commit v3 on v2

--- a/solution.py
+++ b/solution.py
@@ -12,10 +12,10 @@
 CHUNK = 512
 CHUNKS = TOKENS // CHUNK
 BF, F32 = jnp.bfloat16, jnp.float32
-DIRECT = 20
+DIRECT = 22
 RELAYED = (1, 3, 5, 7, 9, 11, 13, 15, 17, 18)
 STRAIGHT = (1, None, 3, 5, 7, 9, 11, None, 13, 14)
-LAST = UNITS - 1 + STRAIGHT[-1]
+LAST = max(UNITS - 1 + STRAIGHT[-1], DIRECT - 1 + RELAYED[-1])
 
 
 def kernel(
@@ -92,7 +92,7 @@
     keep(0, total[...])
 
     def place(u):
-        k = lax.rem(u, 3)
+        k = lax.rem(u + core, 3)
         e0, e1, e2 = lax.div((1 - k) * (2 - k), 2), k * (2 - k), lax.div(k * (k - 1), 2)
         dims = ((cx, 32), (cy, 8), (cz, 2))
         res = []
@@ -259,8 +259,8 @@
         return 0
 
     def tail(t, _):
+        events(t, True)
         events(t, False, UNITS - DIRECT + 1, 99)
-        events(t, True)
         return 0
 
     lax.fori_loop(1, CHUNKS + 1, lambda t, _: loop(t, True, 0, CHUNKS), 0)

time: 125 us -> 123 us (0.984)
  Pallas kernels: 125 us -> 122 us
    pallas_call x1, Pallas kernels: 120 us -> 117 us  [body(): pl.pallas_call(kernel, out_shape=pltpu.VMEM((UNITS, 2, 64, *tile), BF), i...]
where the time goes in v3:
time: 123 us; the launch traced here: 122 us
  Pallas kernels  122 us (99%)
    pallas_call x1, Pallas kernels, body(): pl.pallas_call(kernel, out_shape=pltpu.VMEM((UNITS, 2, 64, *tile), BF), i...  117 us
    pallas_call x1, Pallas kernels, body(): pl.pallas_call(write, out_shape=jax.ShapeDtypeStruct((MATRICES, D // 16,...  5.29 us

profile of v3, /device:TPU:1, one launch (start us, length us, event | category | flops | bytes accessed | tf_op | source)
XLA Modules:
  0.0 122.4 jit_solution(12123467441779295143)
XLA Ops:
  0.0 117.1 %shard_map.28.tb = bf16[26,2,64,16,128]{4,3,2,1,0:T(8,128)(2,1)S(1)} custom-call(bf16[1,2,4096,1024]{3,2,1,0:T(8,128)(2,1)} %a_ref.1, bf16[1,2,4096,3328]{3,2,1,0:T(8,128)(2,1)} %g_ref.1), custom_call_target="tpu_custom_call" | custom-call | flops 55834574848 | bytes 100000000 | tf_op jit(solution)/shard_map/pallas_call | solution.py:288
  117.2 5.3 %shard_map.29 = bf16[2,64,16,3328]{3,2,1,0:T(8,128)(2,1)} custom-call(bf16[26,2,64,16,128]{4,3,2,1,0:T(8,128)(2,1)S(1)} %shard_map.28.tb), custom_call_target="tpu_custom_call" | custom-call | tf_op jit(solution)/shard_map/pallas_call | solution.py:317
